TPU v7x, 128 devices: a whole 4x4x4 slice. The times are simulated.
128 devices in a mesh: rows: 16 (over x, y_lo, core), dim: 8 (over y_hi, z).
Axes of the slice: x: 4, y: 4 (y_hi: 2, y_lo: 2; y = y_hi * 2 + y_lo), z: 4, core: 2. Of those that a mesh axis runs over, the one named last changes fastest.
Arguments:
- entity_table: float32 [524288, 512], P(('rows', 'dim')), may hold values from -2.5 to 2.5
- relations: float32 [822, 512], replicated, may hold values from -6 to 6
- thresholds: float32 [64], replicated, may hold values from 0.2 to 2
- head_ids: int32 [2048], replicated, may hold values from 0 to 524287
- rel_ids: int32 [2048], replicated, may hold values from 0 to 821
- thr_idx: int32 [2048], replicated, may hold values from 0 to 63
Outputs:
- serving_table: float32 [524288, 512], P('rows', 'dim')
- fraction: float32 [2048], P(('rows', 'dim'))
All inputs are finite; a program needn't handle non-finite values.
Results may differ from a plain program's by a relative error of at most 0.0011.
Values sent between devices are 32-bit elements; how exact they have to be, the bound alone decides.
A program may use at most 128 MiB of HBM per device.

v0:
```python
import jax
import jax.numpy as jnp
from jax import lax
from jax.sharding import PartitionSpec as P

sharpness = 2.0


def cut_along(value, dim, length):
    lengths = value.shape
    parts = value.reshape(*lengths[:dim], length, lengths[dim] // length, *lengths[dim + 1 :])
    return jnp.moveaxis(parts, dim, 0)


def cut_rows(length, count):
    lap = length // count
    if lap >= 8:
        lap -= lap % 8
    return [lap * k for k in range(1, count)]


def joined_along(parts, dim):
    lengths = list(parts.shape[1:])
    lengths[dim] *= parts.shape[0]
    return jnp.moveaxis(parts, 0, dim).reshape(lengths)


def several_exchanges(value, axis, pieces, split_dim, concat_dim):
    parts = cut_along(value, split_dim, lax.axis_size(axis))
    cut = max(range(1, max(2, parts.ndim - 1)), key=lambda d: parts.shape[d])
    outs = []
    for slab in jnp.split(parts, cut_rows(parts.shape[cut], pieces), axis=cut):
        if slab.size:
            outs.append(lax.all_to_all(slab, axis, split_axis=0, concat_axis=0, tiled=True))
    return joined_along(jnp.concatenate(outs, axis=cut), concat_dim)


def pick_rows(table, head_ids, start):
    count = table.shape[0]
    local = head_ids - start
    owned = (local >= 0) & (local < count)
    picked = jnp.take(table, jnp.clip(local, 0, count - 1), axis=0)
    return jnp.where(owned[:, None], picked, jnp.zeros_like(picked))


def shards(entity_table, relations, thresholds, head_ids, rel_ids, thr_idx):
    local_rows = entity_table.shape[0]
    width = entity_table.shape[1]
    total_ents = local_rows * lax.axis_size("rows") * lax.axis_size("dim")
    serving = several_exchanges(entity_table, "dim", 2, 1, 0)
    start = (lax.axis_index("rows") * lax.axis_size("dim") + lax.axis_index("dim")) * local_rows
    partial_value = pick_rows(entity_table, head_ids, start)
    head_vecs = lax.psum(partial_value, ("rows", "dim"))
    query = (head_vecs * jnp.take(relations, rel_ids, axis=0)).astype(jnp.bfloat16)
    ent_low = entity_table.astype(jnp.bfloat16)
    level = jnp.take(thresholds, thr_idx)
    queries = query.shape[0]
    query_blocks = query.reshape(queries // 512, 512, width)
    level_blocks = level.reshape(queries // 512, 512)

    def score_block(pair):
        rows_q, rows_level = pair
        score = jnp.dot(rows_q, ent_low.T, preferred_element_type=jnp.float32)
        soft = jax.nn.sigmoid(sharpness * (score - rows_level[:, None]))
        return jnp.sum(soft, axis=1) * (1.0 / total_ents)

    partial_share = lax.map(score_block, (query_blocks, level_blocks)).reshape(queries)
    fraction = lax.psum_scatter(partial_share, ("rows", "dim"), scatter_dimension=0, tiled=True)
    return (serving, fraction)


def solution(mesh):
    placed = (P(("rows", "dim"), None), P(), P(), P(), P(), P())
    return jax.shard_map(
        shards,
        mesh=mesh,
        in_specs=placed,
        out_specs=(P("rows", "dim"), P(("rows", "dim"))),
        check_vma=False,
    )
```

profile of v0, /device:TPU:1, one launch (start us, length us, event | category | flops | bytes accessed | tf_op | source)
XLA Modules:
  0.0 349.4 jit_solution(9521090022698641144)
XLA Ops:
  7.2 0.0 copy-start
  7.2 9.0 %copy.12 = f32[4096,512]{0,1:T(8,128)} copy(f32[4096,512]{1,0:T(8,128)} %param.8) | data formatting | bytes 16777216 | tf_op args[0]
  16.2 7.9 %fusion.6 = (f32[8,2048,64]{1,2,0:T(8,128)}, f32[8,2048,64]{1,2,0:T(8,128)}) fusion(f32[8,4096,64]{1,2,0:T(8,128)} %bitcast.87), kind=kLoop, calls=%fused_computation.21 | loop fusion | bytes 16777216 | tf_op jit(solution)/shard_map/split | solution.py:32
  24.1 0.0 copy-start.4
  24.1 8.6 %all-to-all-start = ((f32[8,2048,64]{1,2,0:T(8,128)}), f32[8,2048,64]{1,2,0:T(8,128)}, u32[]{:S(2)}, u32[]{:S(2)}) async-start(f32[8,2048,64]{1,2,0:T(8,128)} %get-tuple-element.40), calls=%async_computation | async-start | bytes 8388608 | tf_op jit(solution)/shard_map/all_to_all | solution.py:34
  32.7 0.0 all-reduce.3.cloned.1.call-start
  32.7 0.0 copy-done.4
  32.8 12.9 %gather_fusion = f32[2048,512]{1,0:T(8,128)} fusion(f32[4096,512]{1,0:T(8,128)} %param.8, s32[2048]{0:T(1024)S(1)} %fusion.5), kind=kCustom, calls=%fused_computation | custom fusion | bytes 8396800 | tf_op jit(solution)/shard_map/jit(_take)/gather | solution.py:42
  45.7 4.0 %select_select_fusion = f32[2048,512]{1,0:T(8,128)} fusion(f32[2048,512]{1,0:T(8,128)} %gather_fusion, pred[2048]{0:T(1024)(128)(4,1)S(1)} %get-tuple-element.43, pred[2048]{0:T(1024)(128)(4,1)S(1)} %get-tuple-element.42), kind=kLoop, calls=%fused_computation.11 | loop fusion | flops 2097152 | bytes 8392704 | tf_op jit(solution)/shard_map/jit(_where)/select_n | solution.py:43
  49.6 0.0 all-reduce.3.cloned.1.call-update
  49.7 0.0 copy-start.2
  49.7 0.0 copy-start.5
  49.7 0.0 copy-start.3
  49.7 5.9 %convert_element_type.7 = bf16[4096,512]{1,0:T(8,128)(2,1)} convert(f32[4096,512]{1,0:T(8,128)} %param.8) | non-fusion elementwise | flops 2097152 | bytes 12582912 | tf_op jit(solution)/shard_map/convert_element_type | solution.py:55
  55.5 0.0 copy-done.2
  55.5 0.7 fusion.10
  56.2 0.7 fusion.8
  57.0 0.7 fusion.7
  57.7 0.7 fusion.9
  58.4 0.0 copy-done.5
  58.4 39.7 %select_select_fusion.1 = f32[2048]{0:T(1024)S(1)} fusion(s32[2048]{0:T(1024)S(1)} %copy-done.5, f32[]{:T(128)} %bitcast.7, f32[]{:T(128)} %bitcast.8, f32[]{:T(128)} %bitcast.9, f32[]{:T(128)} %bitcast.10, f32[]{:T(128)} %bitcast.11, f32[]{:T(128)} %bitcast.12, f32[]{:T(128)} %bitcast.13, f32[]{:T(128)} %bitcast.14, f32[]{:T(128)} %bitcast.15, f32[]{:T(128)} %bitcast.16, ...), kind=kLoop, calls=%fused_computation.15 | loop fusion | flops 272384 | bytes 16640 | tf_op jit(solution)/shard_map/jit(_take)/select_n | solution.py:56
  98.2 0.0 copy-done.3
  98.2 0.0 copy-done
  98.2 8.9 %gather_fusion.1 = f32[2048,512]{1,0:T(8,128)} fusion(f32[822,512]{1,0:T(8,128)S(1)} %copy-done, s32[2048]{0:T(1024)S(1)} %fusion.4), kind=kCustom, calls=%fused_computation.1 | custom fusion | bytes 8396800 | tf_op jit(solution)/shard_map/jit(_take)/gather | solution.py:54
  107.1 112.8 %all-reduce.3.cloned.1.call-done = f32[2048,512]{1,0:T(8,128)} async-done(((f32[2048,512]{1,0:T(8,128)}), f32[2048,512]{1,0:T(8,128)}) %all-reduce.3.cloned.1.call-update) | async-done | bytes 4194320 | tf_op jit(solution)/shard_map/psum | solution.py:53
  219.9 4.7 %multiply_convert_fusion = bf16[2048,512]{1,0:T(8,128)(2,1)} fusion(f32[2048,512]{1,0:T(8,128)} %all-reduce.3.cloned.1.call-done, f32[2048,512]{1,0:T(8,128)} %gather_fusion.1, pred[2048]{0:T(1024)(128)(4,1)S(1)} %compare_and_fusion), kind=kLoop, calls=%fused_computation.10 | loop fusion | flops 3145728 | bytes 10487808 | tf_op jit(solution)/shard_map/convert_element_type | solution.py:54
  224.6 0.0 all-to-all-done
  224.6 4.7 %all-to-all-start.1 = ((f32[8,2048,64]{1,2,0:T(8,128)}), f32[8,2048,64]{1,2,0:T(8,128)}, u32[]{:S(2)}, u32[]{:S(2)}) async-start(f32[8,2048,64]{1,2,0:T(8,128)} %get-tuple-element.41), calls=%async_computation.1 | async-start | bytes 8388608 | tf_op jit(solution)/shard_map/all_to_all | solution.py:34
  229.4 22.9 %while.10 = (s32[]{:T(128)}, f32[4,512]{1,0:T(4,128)S(1)}, bf16[4,512,512]{2,1,0:T(8,128)(2,1)}, bf16[4096,512]{1,0:T(8,128)(2,1)}, f32[4,512]{1,0:T(4,128)S(1)}, /*index=5*/s32[]{:T(128)}, s32[]{:T(128)}) while((s32[]{:T(128)}, f32[4,512]{1,0:T(4,128)S(1)}, bf16[4,512,512]{2,1,0:T(8,128)(2,1)}, bf16[4096,512]{1,0:T(8,128)(2,1)}, ...), condition=%wide.region_3.4_spmd, body=%wide.region_1.3_spmd.sunk | while | flops 2160066560 | bytes 4735073 | solution.py:67
  229.4 5.6 %fusion.17 = f32[512]{0:T(512)S(1)} fusion(bf16[4096,512]{1,0:T(8,128)(2,1)} %get-tuple-element.156, f32[512]{0:T(512)S(1)} %bitcast.91, bf16[4,512,512]{2,1,0:T(8,128)(2,1)} %get-tuple-element.155, s32[]{:T(128)S(6)} %copy.20), kind=kOutput, calls=%fused_computation.3.clone.1 | convolution fusion | flops 2160066048 | bytes 4722692 | tf_op jit(solution)/shard_map/while/body/eval_jaxpr/dot_general | solution.py:63
  235.1 0.1 dynamic_update_slice.5
  235.1 5.6 %fusion.17 = f32[512]{0:T(512)S(1)} fusion(bf16[4096,512]{1,0:T(8,128)(2,1)} %get-tuple-element.156, f32[512]{0:T(512)S(1)} %bitcast.91, bf16[4,512,512]{2,1,0:T(8,128)(2,1)} %get-tuple-element.155, s32[]{:T(128)S(6)} %copy.20), kind=kOutput, calls=%fused_computation.3.clone.1 | convolution fusion | flops 2160066048 | bytes 4722692 | tf_op jit(solution)/shard_map/while/body/eval_jaxpr/dot_general | solution.py:63
  240.8 0.1 dynamic_update_slice.5
  240.9 5.6 %fusion.17 = f32[512]{0:T(512)S(1)} fusion(bf16[4096,512]{1,0:T(8,128)(2,1)} %get-tuple-element.156, f32[512]{0:T(512)S(1)} %bitcast.91, bf16[4,512,512]{2,1,0:T(8,128)(2,1)} %get-tuple-element.155, s32[]{:T(128)S(6)} %copy.20), kind=kOutput, calls=%fused_computation.3.clone.1 | convolution fusion | flops 2160066048 | bytes 4722692 | tf_op jit(solution)/shard_map/while/body/eval_jaxpr/dot_general | solution.py:63
  246.5 0.1 dynamic_update_slice.5
  246.6 5.6 %fusion.17 = f32[512]{0:T(512)S(1)} fusion(bf16[4096,512]{1,0:T(8,128)(2,1)} %get-tuple-element.156, f32[512]{0:T(512)S(1)} %bitcast.91, bf16[4,512,512]{2,1,0:T(8,128)(2,1)} %get-tuple-element.155, s32[]{:T(128)S(6)} %copy.20), kind=kOutput, calls=%fused_computation.3.clone.1 | convolution fusion | flops 2160066048 | bytes 4722692 | tf_op jit(solution)/shard_map/while/body/eval_jaxpr/dot_general | solution.py:63
  252.3 0.1 dynamic_update_slice.5
  252.4 81.6 %all-reduce = f32[2048]{0:T(1024)S(1)} all-reduce(f32[2048]{0:T(1024)S(1)} %bitcast.92), channel_id=2, replica_groups=mesh['rows'=16,'dim'=8] {'rows','dim'}, use_global_device_ids=true, to_apply=%region_4.5.clone | all-reduce | flops 2048 | bytes 16384
  334.0 0.6 dynamic-slice
  334.6 0.0 all-to-all-done.1
  334.6 4.0 %maximum_bitcast_fusion = f32[8,8,8,4096]{3,2,1,0:T(8,128)S(1)} fusion(f32[8,2048,64]{1,2,0:T(8,128)} %all-to-all-done.1, f32[8,2048,64]{1,2,0:T(8,128)} %all-to-all-done), kind=kLoop, calls=%fused_computation.9 | loop fusion | flops 2097152 | bytes 16777216
  338.6 0.0 copy-start.1
  338.6 3.9 %copy.14 = f32[8,8,8,4096]{3,2,0,1:T(8,128)} copy(f32[8,8,8,4096]{3,2,1,0:T(8,128)S(1)} %maximum_bitcast_fusion) | data formatting | bytes 16777216 | tf_op jit(solution)/shard_map/reshape | solution.py:25
  342.5 0.0 copy-done.1
  (15 shorter events, 0.1 us)
Async XLA Ops:
  7.2 91.0 %copy-start = (f32[822,512]{1,0:T(8,128)S(1)}, f32[822,512]{1,0:T(8,128)}, u32[]{:S(2)}) copy-start(f32[822,512]{1,0:T(8,128)} %param.9) | copy-start | bytes 5050372
  24.1 8.7 %copy-start.4 = (s32[2048]{0:T(1024)S(1)}, s32[2048]{0:T(1024)}, u32[]{:S(2)}) copy-start(s32[2048]{0:T(1024)} %param.11) | copy-start | bytes 24580
  24.1 200.6 %all-to-all-start = ((f32[8,2048,64]{1,2,0:T(8,128)}), f32[8,2048,64]{1,2,0:T(8,128)}, u32[]{:S(2)}, u32[]{:S(2)}) async-start(f32[8,2048,64]{1,2,0:T(8,128)} %get-tuple-element.40), calls=%async_computation | async-start | bytes 8388608 | tf_op jit(solution)/shard_map/all_to_all | solution.py:34
  32.7 187.2 %all-reduce.3.cloned.1.call-start = ((), (), s32[]{:S(2)}) async-start(), calls=%async_computation.2 | async-start | bytes 8388608 | tf_op jit(solution)/shard_map/psum | solution.py:53
  49.7 5.9 %copy-start.2 = (f32[64]{0:T(128)S(1)}, f32[64]{0:T(128)}, u32[]{:S(2)}) copy-start(f32[64]{0:T(128)} %param.10) | copy-start | bytes 772
  49.7 8.7 %copy-start.5 = (s32[2048]{0:T(1024)S(1)}, s32[2048]{0:T(1024)}, u32[]{:S(2)}) copy-start(s32[2048]{0:T(1024)} %param.13) | copy-start | bytes 24580
  49.7 48.5 %copy-start.3 = (s32[2048]{0:T(1024)S(1)}, s32[2048]{0:T(1024)}, u32[]{:S(2)}) copy-start(s32[2048]{0:T(1024)} %param.12) | copy-start | bytes 24580
  224.6 109.9 %all-to-all-start.1 = ((f32[8,2048,64]{1,2,0:T(8,128)}), f32[8,2048,64]{1,2,0:T(8,128)}, u32[]{:S(2)}, u32[]{:S(2)}) async-start(f32[8,2048,64]{1,2,0:T(8,128)} %get-tuple-element.41), calls=%async_computation.1 | async-start | bytes 8388608 | tf_op jit(solution)/shard_map/all_to_all | solution.py:34
  338.6 4.0 %copy-start.1 = (f32[822,512]{1,0:T(8,128)S(1)}, f32[822,512]{1,0:T(8,128)}, u32[]{:S(2)}) copy-start(f32[822,512]{1,0:T(8,128)} %param.9) | copy-start | bytes 5050372
Sparse Core Ops, SparseCore 0:
  49.8 170.1 all-reduce.2
where the time goes:
time: 351 us; the launch traced here: 349 us
  waiting for transfers between devices  113 us (32%)
  blocking collectives  81.6 us (23%)
  other arithmetic  58.3 us (17%)
  local copies, waits for them, and re-layouts  46.3 us (13%)
  matrix products  22.6 us (6%)
  between operations  14.2 us (4%)
  starting transfers between devices  13.4 us (4%)
    psum x1, waiting for transfers between devices, shards(): head_vecs = lax.psum(partial_value, ('rows', 'dim'))  113 us
    unnamed x1, blocking collectives  81.6 us
    select_n x1, other arithmetic, shards(): level = jnp.take(thresholds, thr_idx)  39.7 us
    dot_general x4, matrix products, score_block(): score = jnp.dot(rows_q, ent_low.T, preferred_element_type=jnp.float32)  22.6 us
    all_to_all x2, starting transfers between devices, several_exchanges(): lax.all_to_all(slab, axis, split_axis=0, concat_axis=0, tiled=True)  13.4 us
    gather x1, local copies, waits for them, and re-layouts, pick_rows(): picked = jnp.take(table, jnp.clip(local, 0, count - 1), axis=0)  12.9 us
    unnamed x15, local copies, waits for them, and re-layouts  9.66 us
    gather x1, local copies, waits for them, and re-layouts, shards(): jnp.take(relations, rel_ids, axis=0)  8.9 us
  transfers between devices with their start and end apart: 3, of which 1 were waited for; matrix products, arithmetic and copies ran while one was open for 29% of the time, Pallas kernels for 0%

commit v1 on v0

v1 whole, which is shorter than its diff:
```python
import functools

import jax
import jax.numpy as jnp
from jax import lax
from jax.experimental import pallas as pl
from jax.experimental.pallas import tpu as pltpu
from jax.sharding import PartitionSpec as P

MESH = pl.DeviceIdType.MESH
F32 = jnp.float32
sharpness = 2.0

PLANE = [(a, b, z) for a in range(2) for b in range(2) for z in range(4)][1:]
SLABS = [(0, 0, 1), (0, 0, 3), (0, 1, 0), (0, 0, 2), (0, 1, 1), (0, 1, 3), (0, 1, 2)]
WAVES = [(0, 1152), (1152, 256), (1408, 1792), (3200, 896)]


def kernel(
    total_ents, head_ids, rel_ids, thresholds, table, relations, thr_idx,
    serving, share,
    tab, tab_t, ent, rel, theirs, mine, pair_in, x_in, plane_in, rel_rows, query_rows, queries,
    level, totals, pair_tot, x_tot, plane_tot,
    load_sem, own_sem, slab_send, slab_recv, pair_send, pair_recv, x_send, x_recv,
    plane_send, plane_recv, gath_send, gath_recv, xg_send, xg_recv, pg_send, pg_recv,
    tot_send, tot_recv,
):
    r, d = lax.axis_index("rows"), lax.axis_index("dim")
    x, y_lo, core = r // 4, (r // 2) % 2, r % 2
    y_hi, z = d // 4, d % 4
    ents = table.shape[0]
    width = table.shape[1]
    group = x_in.shape[1]
    slab = serving.shape[0]

    def at_plane(off):
        a, b, dz = off
        row = x * 4 + ((y_lo + a) % 2) * 2 + core
        return row, ((y_hi + b) % 2) * 4 + (z + dz) % 4

    def at_x(k):
        return ((x + k) % 4) * 4 + y_lo * 2 + core, d

    partner = (x * 4 + y_lo * 2 + (1 - core), d)

    def send(src, dst, s, t, peer):
        copy = pltpu.make_async_remote_copy(
            src_ref=src, dst_ref=dst, send_sem=s, recv_sem=t, device_id=peer, device_id_type=MESH
        )
        copy.start()
        return copy

    cuts = [0, WAVES[0][1], 2048, 3072, ents]
    loads = []
    for k in range(4):
        span = pl.ds(cuts[k], cuts[k + 1] - cuts[k])
        loads.append(pltpu.make_async_copy(table.at[span], tab.at[span], load_sem.at[k]))
        loads[-1].start()
    load_rel = pltpu.make_async_copy(relations, rel, load_sem.at[4])
    load_rel.start()
    barrier = pltpu.get_barrier_semaphore()
    peers = [at_plane(off) for off in PLANE] + [at_x(k) for k in (1, 2, 3)] + [partner]
    for peer in peers:
        pl.semaphore_signal(barrier, inc=1, device_id=peer, device_id_type=MESH)

    def transpose_rows(first, count):
        @pl.loop(0, count // 128)
        def _(i):
            span = pl.ds(pl.multiple_of(first + i * 128, 128), 128)
            tab_t[:, span] = tab[span, :].T

    slab_copies, own_copies = [], []

    def start_wave(w):
        first, count = WAVES[w]
        span = pl.ds(first, count)
        here = pl.ds(pl.multiple_of(d * ents + first, 128), count)
        for i, off in enumerate(SLABS):
            row, col = at_plane(off)
            rows = pl.ds(pl.multiple_of(col * slab, 8), slab)
            slab_copies.append(
                send(tab_t.at[rows, span], serving.at[:, here], slab_send.at[w, i], slab_recv.at[w, i], (row, col))
            )
        rows = pl.ds(pl.multiple_of(d * slab, 8), slab)
        own = pltpu.make_async_copy(tab_t.at[rows, span], serving.at[:, here], own_sem.at[w])
        own.start()
        own_copies.append(own)

    loads[0].wait()
    transpose_rows(*WAVES[0])
    pl.semaphore_wait(barrier, len(peers))
    start_wave(0)
    for k in range(1, 4):
        loads[k].wait()

    start = (r * lax.axis_size("dim") + d) * ents

    def pick(out, half):
        def part(k):
            @pl.loop(0, group // 8)
            def _(i):
                for j in range(8):
                    low = i * 8 + j
                    q = k * 512 + (low // 128) * 256 + half * 128 + low % 128
                    local = head_ids[q] - start
                    owned = jnp.logical_and(local >= 0, local < ents)
                    row = tab[pl.ds(jnp.clip(local, 0, ents - 1), 1), :]
                    out[k, pl.ds(low, 1), :] = jnp.where(owned, row, jnp.zeros_like(row))
        return part

    order = [(x + 2) % 4, (x + 1) % 4, (x + 3) % 4, x]
    copies = []
    for n in range(4):
        pick(theirs, 1 - core)(order[n])
        copies.append(send(theirs.at[order[n]], pair_in.at[order[n]], pair_send.at[n], pair_recv.at[n], partner))
    for n in range(4):
        pick(mine, core)(order[n])

    x_copies = {}
    for n, k in enumerate((2, 1, 3, 0)):
        copies[n].wait_recv()
        mine[order[n]] += pair_in[order[n]]
        if k:
            x_copies[k] = send(mine.at[order[n]], x_in.at[k - 1], x_send.at[k - 1], x_recv.at[k - 1], at_x(k))

    transpose_rows(WAVES[0][1], ents - WAVES[0][1])

    @pl.loop(0, ents // 256)
    def _(i):
        span = pl.ds(pl.multiple_of(i * 256, 256), 256)
        ent[span, :] = tab[span, :].astype(jnp.bfloat16)

    found = jnp.zeros(level.shape, F32)
    for k in range(thresholds.shape[0]):
        found = jnp.where(thr_idx[...] == k, thresholds[k], found)
    level[...] = found
    load_rel.wait()
    first_q = r * 128 + d * 16
    for i in range(16):
        rel_rows[pl.ds(i, 1), :] = rel[pl.ds(rel_ids[first_q + i], 1), :]

    for k in (1, 3, 2):
        x_copies[k].wait_recv()
        mine[x] += x_in[k - 1]

    def rows_of(row, col):
        return pl.ds(pl.multiple_of(((row // 2) % 2) * 128 + col * 16, 16), 16)

    plane_copies = []
    for i, off in enumerate(PLANE):
        peer = at_plane(off)
        plane_copies.append(
            send(mine.at[x, rows_of(*peer)], plane_in.at[i], plane_send.at[i], plane_recv.at[i], peer)
        )
    start_wave(1)
    head = mine[x, rows_of(r, d)]
    for i in range(15):
        plane_copies[i].wait_recv()
        head += plane_in[i]

    query_rows[...] = (head * rel_rows[...]).astype(jnp.bfloat16).astype(F32)
    own_group = core * 4 + x
    gath_copies = []
    for i, off in enumerate(PLANE):
        gath_copies.append(
            send(query_rows, queries.at[own_group, rows_of(r, d)], gath_send.at[i], gath_recv.at[i], at_plane(off))
        )
    start_wave(2)
    queries[own_group, rows_of(r, d)] = query_rows[...]
    for i in range(15):
        gath_copies[i].wait_recv()

    xg_copies = {}
    for k in (1, 3, 2):
        xg_copies[k] = send(queries.at[own_group], queries.at[own_group], xg_send.at[k - 1], xg_recv.at[k - 1], at_x(k))

    tile = 512

    def count(half, k):
        g = half * 4 + k
        low = queries[g].astype(jnp.bfloat16)
        lev = jnp.concatenate(
            [level[pl.ds(k * 4 + half, 1), :], level[pl.ds(k * 4 + 2 + half, 1), :]], axis=1
        )

        def step(i, acc):
            rows = ent[pl.ds(pl.multiple_of(i * tile, tile), tile), :]
            score = lax.dot_general(rows, low, (((1,), (1,)), ((), ())), preferred_element_type=F32)
            soft = 1.0 / (1.0 + jnp.exp(sharpness * (lev - score)))
            return acc + jnp.sum(soft.reshape(tile // 8, 8, group), axis=0)

        totals[g] = lax.fori_loop(0, ents // tile, step, jnp.zeros((8, group), F32))

    pg_copies = []
    for n, k in enumerate((0, 1, 3, 2)):
        from_x = (x + 4 - k) % 4
        if k:
            xg_copies[k].wait_recv()
        g = core * 4 + from_x
        pg_copies.append(send(queries.at[g], queries.at[g], pg_send.at[n], pg_recv.at[n], partner))
        count(core, from_x)
        pg_copies[n].wait_recv()
        count(1 - core, from_x)

    other = pl.ds((1 - core) * 4, 4)
    half = send(totals.at[other], pair_tot, tot_send.at[0], tot_recv.at[0], partner)
    half.wait_recv()
    x_tots = {}
    for k in (0, 1, 2, 3):
        to = (x + k) % 4
        x_tot[k] = totals[core * 4 + to] + pair_tot[to]
        if k:
            x_tots[k] = send(x_tot.at[k], x_tot.at[3 + k], tot_send.at[k], tot_recv.at[k], at_x(k))
    sums = x_tot[0]
    for k in (1, 2, 3):
        x_tots[k].wait_recv()
        sums += x_tot[3 + k]
    plane_tot[0] = sums[:, :128]
    plane_tot[1] = sums[:, 128:]
    plane_tots = []
    for i, off in enumerate(PLANE):
        row, col = at_plane(off)
        plane_tots.append(
            send(plane_tot.at[(row // 2) % 2], plane_tot.at[2 + i], tot_send.at[4 + i], tot_recv.at[4 + i], (row, col))
        )
    start_wave(3)
    whole = plane_tot[y_lo]
    for i in range(15):
        plane_tots[i].wait_recv()
        whole += plane_tot[2 + i]
    whole = jnp.sum(whole, axis=0, keepdims=True) * (1.0 / total_ents)
    share[...] = pltpu.roll(jnp.broadcast_to(whole, (8, 128)), (128 - d * 16) % 128, 1)

    for copy in slab_copies:
        copy.wait_recv()
    for copy in own_copies:
        copy.wait()
    sent = copies + list(x_copies.values()) + plane_copies + gath_copies + list(xg_copies.values())
    for copy in sent + pg_copies + [half] + list(x_tots.values()) + plane_tots + slab_copies:
        copy.wait_send()


def shards(entity_table, relations, thresholds, head_ids, rel_ids, thr_idx):
    ents, width = entity_table.shape
    n_rows, n_dim = lax.axis_size("rows"), lax.axis_size("dim")
    total_ents = ents * n_rows * n_dim
    slab = width // n_dim
    group = 256
    hbm = pl.BlockSpec(memory_space=pl.ANY)
    smem = pl.BlockSpec(memory_space=pltpu.SMEM)
    vmem = pl.BlockSpec(memory_space=pltpu.VMEM)
    dma = pltpu.SemaphoreType.DMA
    waves = len(WAVES)
    serving, share = pl.pallas_call(
        functools.partial(kernel, total_ents),
        out_shape=(
            jax.ShapeDtypeStruct((slab, ents * n_dim), F32),
            jax.ShapeDtypeStruct((8, 128), F32),
        ),
        in_specs=[smem, smem, smem, hbm, hbm, vmem],
        out_specs=(hbm, vmem),
        scratch_shapes=[
            pltpu.VMEM((ents, width), F32),
            pltpu.VMEM((width, ents), F32),
            pltpu.VMEM((ents, width), jnp.bfloat16),
            pltpu.VMEM(relations.shape, F32),
            pltpu.VMEM((4, group, width), F32),
            pltpu.VMEM((4, group, width), F32),
            pltpu.VMEM((4, group, width), F32),
            pltpu.VMEM((3, group, width), F32),
            pltpu.VMEM((15, 16, width), F32),
            pltpu.VMEM((16, width), F32),
            pltpu.VMEM((16, width), F32),
            pltpu.VMEM((8, group, width), F32),
            pltpu.VMEM((16, 128), F32),
            pltpu.VMEM((8, 8, group), F32),
            pltpu.VMEM((4, 8, group), F32),
            pltpu.VMEM((7, 8, group), F32),
            pltpu.VMEM((17, 8, 128), F32),
            dma((5,)),
            dma((waves,)),
            dma((waves, 7)), dma((waves, 7)),
            dma((4,)), dma((4,)),
            dma((3,)), dma((3,)),
            dma((15,)), dma((15,)),
            dma((15,)), dma((15,)),
            dma((3,)), dma((3,)),
            dma((4,)), dma((4,)),
            dma((19,)), dma((19,)),
        ],
        compiler_params=pltpu.CompilerParams(
            collective_id=0, has_side_effects=True, vmem_limit_bytes=60 * 1024 * 1024
        ),
        name="serve_and_count",
    )(head_ids, rel_ids, thresholds, entity_table, relations, thr_idx.reshape(16, 128))
    return serving.T, share[0, :16]


def solution(mesh):
    placed = (P(("rows", "dim"), None), P(), P(), P(), P(), P())
    return jax.shard_map(
        shards,
        mesh=mesh,
        in_specs=placed,
        out_specs=(P("rows", "dim"), P(("rows", "dim"))),
        check_vma=False,
    )
```

time: 351 us -> 157 us (0.45)
  Pallas kernels: 0 us -> 148 us
  waiting for transfers between devices: 113 us -> 0 us
  blocking collectives: 81.6 us -> 0 us
  other arithmetic: 58.3 us -> 0 us
  local copies, waits for them, and re-layouts: 46.3 us -> 8.58 us
  matrix products: 22.6 us -> 0 us
  between operations: 14.2 us -> 0.64 us
  starting transfers between devices: 13.4 us -> 0 us
    pallas_call x0 -> x1, Pallas kernels: none -> 148 us  [shards(): pl.pallas_call(functools.partial(kernel, total_ents), out_shape=(jax.Shap...]
    psum x1 -> x0, waiting for transfers between devices: 113 us -> none  [shards(): head_vecs = lax.psum(partial_value, ('rows', 'dim'))]
    unnamed x1 -> x0, blocking collectives: 81.6 us -> none
    select_n x2 -> x0, other arithmetic: 43.7 us -> none  [the longest x1 39.7 us: shards(): level = jnp.take(thresholds, thr_idx)]
    gather x6 -> x0, local copies, waits for them, and re-layouts: 24.6 us -> none  [the longest x1 12.9 us: pick_rows(): picked = jnp.take(table, jnp.clip(local, 0, count - 1), axis=0)]
    dot_general x4 -> x0, matrix products: 22.6 us -> none  [score_block(): score = jnp.dot(rows_q, ent_low.T, preferred_element_type=jnp.float32)]
    all_to_all x2 -> x0, starting transfers between devices: 13.4 us -> none  [several_exchanges(): lax.all_to_all(slab, axis, split_axis=0, concat_axis=0, tiled=True)]
    convert_element_type x2 -> x0, other arithmetic: 10.6 us -> none  [the longest x1 5.86 us: shards(): ent_low = entity_table.astype(jnp.bfloat16)]
  transfers between devices with their start and end apart: 3 -> 0, of which waited for: 1 -> 0; matrix products, arithmetic and copies ran while one was open for 29% -> 0% of each run, Pallas kernels for 0% -> 0%
where the time goes in v1:
time: 157 us
  Pallas kernels  148 us (94%)
  local copies, waits for them, and re-layouts  8.58 us (5%)
    pallas_call x1, Pallas kernels, shards(): pl.pallas_call(functools.partial(kernel, total_ents), out_shape=(jax.Shap...  148 us
    unnamed x1, local copies, waits for them, and re-layouts  7.38 us

profile of v1, /device:TPU:1, one launch (start us, length us, event | category | flops | bytes accessed | tf_op | source)
XLA Modules:
  0.0 157.2 jit_solution(18219007974047941979)
XLA Ops:
  0.6 148.0 %serve_and_count.1 = (f32[64,32768]{1,0:T(8,128)}, f32[8,128]{1,0:T(8,128)}) custom-call(s32[2048]{0:T(1024)} %head_ids.1, s32[2048]{0:T(1024)} %rel_ids.1, f32[64]{0:T(128)} %thresholds.1, f32[4096,512]{1,0:T(8,128)} %table.1, f32[822,512]{1,0:T(8,128)} %relations.1, s32[16,128]{1,0:T(8,128)} %bitcast.5), custom_call_target="tpu_custom_call" | custom-call | tf_op jit(solution)/shard_map/serve_and_count/pallas_call | solution.py:254
  148.6 1.2 slice_bitcast_fusion
  149.8 7.4 %copy.9 = f32[32768,64]{0,1:T(8,128)} copy(f32[32768,64]{0,1:T(8,128)} %bitcast.4) | data formatting | bytes 16777216

commit v2 on v1

--- a/solution.py
+++ b/solution.py
@@ -13,7 +13,7 @@
 
 PLANE = [(a, b, z) for a in range(2) for b in range(2) for z in range(4)][1:]
 SLABS = [(0, 0, 1), (0, 0, 3), (0, 1, 0), (0, 0, 2), (0, 1, 1), (0, 1, 3), (0, 1, 2)]
-WAVES = [(0, 1152), (1152, 256), (1408, 1792), (3200, 896)]
+WAVES = [(0, 1152), (1152, 256), (1408, 1920), (3328, 768)]
 
 
 def kernel(
@@ -21,7 +21,7 @@
     serving, share,
     tab, tab_t, ent, rel, theirs, mine, pair_in, x_in, plane_in, rel_rows, query_rows, queries,
     level, totals, pair_tot, x_tot, plane_tot,
-    load_sem, own_sem, slab_send, slab_recv, pair_send, pair_recv, x_send, x_recv,
+    load_sem, slab_send, slab_recv, pair_send, pair_recv, x_send, x_recv,
     plane_send, plane_recv, gath_send, gath_recv, xg_send, xg_recv, pg_send, pg_recv,
     tot_send, tot_recv,
 ):
@@ -69,7 +69,7 @@
             span = pl.ds(pl.multiple_of(first + i * 128, 128), 128)
             tab_t[:, span] = tab[span, :].T
 
-    slab_copies, own_copies = [], []
+    slab_copies = []
 
     def start_wave(w):
         first, count = WAVES[w]
@@ -82,9 +82,7 @@
                 send(tab_t.at[rows, span], serving.at[:, here], slab_send.at[w, i], slab_recv.at[w, i], (row, col))
             )
         rows = pl.ds(pl.multiple_of(d * slab, 8), slab)
-        own = pltpu.make_async_copy(tab_t.at[rows, span], serving.at[:, here], own_sem.at[w])
-        own.start()
-        own_copies.append(own)
+        serving[:, here] = tab_t[rows, span]
 
     loads[0].wait()
     transpose_rows(*WAVES[0])
@@ -94,34 +92,36 @@
         loads[k].wait()
 
     start = (r * lax.axis_size("dim") + d) * ents
-
-    def pick(out, half):
-        def part(k):
-            @pl.loop(0, group // 8)
-            def _(i):
-                for j in range(8):
-                    low = i * 8 + j
-                    q = k * 512 + (low // 128) * 256 + half * 128 + low % 128
-                    local = head_ids[q] - start
-                    owned = jnp.logical_and(local >= 0, local < ents)
-                    row = tab[pl.ds(jnp.clip(local, 0, ents - 1), 1), :]
-                    out[k, pl.ds(low, 1), :] = jnp.where(owned, row, jnp.zeros_like(row))
-        return part
+    tab[pl.ds(ents, 8), :] = jnp.zeros((8, width), F32)
+
+    def pick(out, half, k):
+        @pl.loop(0, group // 8)
+        def _(i):
+            rows = []
+            for j in range(8):
+                low = i * 8 + j
+                q = k * 512 + (low // 128) * 256 + half * 128 + low % 128
+                local = head_ids[q] - start
+                missing = jnp.logical_or(local < 0, local >= ents)
+                rows.append(tab[pl.ds(jnp.where(missing, ents, local), 1), :])
+            out[k, pl.ds(pl.multiple_of(i * 8, 8), 8), :] = jnp.concatenate(rows, axis=0)
 
     order = [(x + 2) % 4, (x + 1) % 4, (x + 3) % 4, x]
-    copies = []
-    for n in range(4):
-        pick(theirs, 1 - core)(order[n])
-        copies.append(send(theirs.at[order[n]], pair_in.at[order[n]], pair_send.at[n], pair_recv.at[n], partner))
-    for n in range(4):
-        pick(mine, core)(order[n])
-
-    x_copies = {}
-    for n, k in enumerate((2, 1, 3, 0)):
+    copies, x_copies = [], {}
+
+    def sum_pair(n, k):
         copies[n].wait_recv()
         mine[order[n]] += pair_in[order[n]]
         if k:
             x_copies[k] = send(mine.at[order[n]], x_in.at[k - 1], x_send.at[k - 1], x_recv.at[k - 1], at_x(k))
+
+    for n, k in enumerate((2, 1, 3, 0)):
+        pick(theirs, 1 - core, order[n])
+        copies.append(send(theirs.at[order[n]], pair_in.at[order[n]], pair_send.at[n], pair_recv.at[n], partner))
+        if n:
+            sum_pair(n - 1, (2, 1, 3, 0)[n - 1])
+        pick(mine, core, order[n])
+    sum_pair(3, 0)
 
     transpose_rows(WAVES[0][1], ents - WAVES[0][1])
 
@@ -233,11 +233,20 @@
 
     for copy in slab_copies:
         copy.wait_recv()
-    for copy in own_copies:
-        copy.wait()
     sent = copies + list(x_copies.values()) + plane_copies + gath_copies + list(xg_copies.values())
     for copy in sent + pg_copies + [half] + list(x_tots.values()) + plane_tots + slab_copies:
         copy.wait_send()
+
+
+def write_out(landed, share, serving, fraction, sems):
+    copies = []
+    for i in range(8):
+        rows = pl.ds(i * (landed.shape[0] // 8), landed.shape[0] // 8)
+        copies.append(pltpu.make_async_copy(landed.at[rows], serving.at[rows], sems.at[i]))
+        copies[-1].start()
+    fraction[...] = share[0, :16]
+    for copy in copies:
+        copy.wait()
 
 
 def shards(entity_table, relations, thresholds, head_ids, rel_ids, thr_idx):
@@ -251,16 +260,16 @@
     vmem = pl.BlockSpec(memory_space=pltpu.VMEM)
     dma = pltpu.SemaphoreType.DMA
     waves = len(WAVES)
-    serving, share = pl.pallas_call(
+    landed, share = pl.pallas_call(
         functools.partial(kernel, total_ents),
         out_shape=(
-            jax.ShapeDtypeStruct((slab, ents * n_dim), F32),
-            jax.ShapeDtypeStruct((8, 128), F32),
+            pltpu.VMEM((slab, ents * n_dim), F32),
+            pltpu.VMEM((8, 128), F32),
         ),
         in_specs=[smem, smem, smem, hbm, hbm, vmem],
-        out_specs=(hbm, vmem),
+        out_specs=(vmem, vmem),
         scratch_shapes=[
-            pltpu.VMEM((ents, width), F32),
+            pltpu.VMEM((ents + 8, width), F32),
             pltpu.VMEM((width, ents), F32),
             pltpu.VMEM((ents, width), jnp.bfloat16),
             pltpu.VMEM(relations.shape, F32),
@@ -278,7 +287,6 @@
             pltpu.VMEM((7, 8, group), F32),
             pltpu.VMEM((17, 8, 128), F32),
             dma((5,)),
-            dma((waves,)),
             dma((waves, 7)), dma((waves, 7)),
             dma((4,)), dma((4,)),
             dma((3,)), dma((3,)),
@@ -289,11 +297,23 @@
             dma((19,)), dma((19,)),
         ],
         compiler_params=pltpu.CompilerParams(
-            collective_id=0, has_side_effects=True, vmem_limit_bytes=60 * 1024 * 1024
+            collective_id=0, has_side_effects=True, vmem_limit_bytes=48 * 1024 * 1024
         ),
         name="serve_and_count",
     )(head_ids, rel_ids, thresholds, entity_table, relations, thr_idx.reshape(16, 128))
-    return serving.T, share[0, :16]
+    serving, fraction = pl.pallas_call(
+        write_out,
+        out_shape=(
+            jax.ShapeDtypeStruct((slab, ents * n_dim), F32),
+            jax.ShapeDtypeStruct((16,), F32),
+        ),
+        in_specs=[vmem, vmem],
+        out_specs=(hbm, vmem),
+        scratch_shapes=[dma((8,))],
+        compiler_params=pltpu.CompilerParams(vmem_limit_bytes=1024 * 1024),
+        name="write_out",
+    )(landed, share)
+    return serving.T, fraction
 
 
 def solution(mesh):

time: 157 us -> 136 us (0.87); the launches traced: 157 us -> 133 us
  Pallas kernels: 148 us -> 132 us
  local copies, waits for them, and re-layouts: 8.58 us -> 0 us
    pallas_call x1 -> x2, Pallas kernels: 148 us -> 132 us  [the longest x1 128 us: shards(): pl.pallas_call(functools.partial(kernel, total_ents), out_shape=(pltpu.VM...]
    unnamed x1 -> x0, local copies, waits for them, and re-layouts: 7.38 us -> none
where the time goes in v2:
time: 136 us; the launch traced here: 133 us
  Pallas kernels  132 us (97%)
    pallas_call x1, Pallas kernels, shards(): pl.pallas_call(functools.partial(kernel, total_ents), out_shape=(pltpu.VM...  128 us
    pallas_call x1, Pallas kernels, shards(): pl.pallas_call(write_out, out_shape=(jax.ShapeDtypeStruct((slab, ents * n...  3.88 us

profile of v2, /device:TPU:1, one launch (start us, length us, event | category | flops | bytes accessed | tf_op | source)
XLA Modules:
  0.0 132.8 jit_solution(4263997228094697500)
XLA Ops:
  0.6 128.3 %serve_and_count.1 = (f32[64,32768]{1,0:T(8,128)S(1)}, f32[8,128]{1,0:T(8,128)S(1)}) custom-call(s32[2048]{0:T(1024)} %head_ids.1, s32[2048]{0:T(1024)} %rel_ids.1, f32[64]{0:T(128)} %thresholds.1, f32[4096,512]{1,0:T(8,128)} %table.1, f32[822,512]{1,0:T(8,128)} %relations.1, s32[16,128]{1,0:T(8,128)} %bitcast.2), custom_call_target="tpu_custom_call" | custom-call | tf_op jit(solution)/shard_map/serve_and_count/pallas_call | solution.py:263
  128.9 3.9 %write_out.1 = (f32[64,32768]{1,0:T(8,128)}, f32[16]{0:T(128)}) custom-call(f32[64,32768]{1,0:T(8,128)S(1)} %get-tuple-element.6.landed, f32[8,128]{1,0:T(8,128)S(1)} %get-tuple-element.7.share), custom_call_target="tpu_custom_call" | custom-call | tf_op jit(solution)/shard_map/write_out/pallas_call | solution.py:304

commit v3 on v2

--- a/solution.py
+++ b/solution.py
@@ -12,13 +12,15 @@
 sharpness = 2.0
 
 PLANE = [(a, b, z) for a in range(2) for b in range(2) for z in range(4)][1:]
-SLABS = [(0, 0, 1), (0, 0, 3), (0, 1, 0), (0, 0, 2), (0, 1, 1), (0, 1, 3), (0, 1, 2)]
-WAVES = [(0, 1152), (1152, 256), (1408, 1920), (3328, 768)]
+SLABS = [(0, 1, 2), (0, 0, 2), (0, 1, 1), (0, 1, 3), (0, 1, 0), (0, 0, 1), (0, 0, 3)]
+COUNTS = [1152, 256, 256, 768, 128, 256, 128, 128, 256, 128, 128, 256, 256]
+WAVES = [(sum(COUNTS[:k]), COUNTS[k]) for k in range(len(COUNTS))]
 
 
 def kernel(
-    total_ents, head_ids, rel_ids, thresholds, table, relations, thr_idx,
+    total_ents, head_ids_in, rel_ids_in, thresholds_in, table, relations, thr_idx_in,
     serving, share,
+    head_ids, rel_ids, thresholds, thr_idx,
     tab, tab_t, ent, rel, theirs, mine, pair_in, x_in, plane_in, rel_rows, query_rows, queries,
     level, totals, pair_tot, x_tot, plane_tot,
     load_sem, slab_send, slab_recv, pair_send, pair_recv, x_send, x_recv,
@@ -50,14 +52,18 @@
         copy.start()
         return copy
 
-    cuts = [0, WAVES[0][1], 2048, 3072, ents]
+    cuts = [0, COUNTS[0], 2048, 3072, ents]
     loads = []
     for k in range(4):
         span = pl.ds(cuts[k], cuts[k + 1] - cuts[k])
         loads.append(pltpu.make_async_copy(table.at[span], tab.at[span], load_sem.at[k]))
         loads[-1].start()
-    load_rel = pltpu.make_async_copy(relations, rel, load_sem.at[4])
-    load_rel.start()
+    small = []
+    for i, (src, dst) in enumerate(
+        ((head_ids_in, head_ids), (rel_ids_in, rel_ids), (thresholds_in, thresholds), (thr_idx_in, thr_idx), (relations, rel))
+    ):
+        small.append(pltpu.make_async_copy(src, dst, load_sem.at[4 + i]))
+        small[-1].start()
     barrier = pltpu.get_barrier_semaphore()
     peers = [at_plane(off) for off in PLANE] + [at_x(k) for k in (1, 2, 3)] + [partner]
     for peer in peers:
@@ -90,21 +96,24 @@
     start_wave(0)
     for k in range(1, 4):
         loads[k].wait()
+    small[0].wait()
 
     start = (r * lax.axis_size("dim") + d) * ents
     tab[pl.ds(ents, 8), :] = jnp.zeros((8, width), F32)
 
     def pick(out, half, k):
-        @pl.loop(0, group // 8)
-        def _(i):
-            rows = []
-            for j in range(8):
-                low = i * 8 + j
-                q = k * 512 + (low // 128) * 256 + half * 128 + low % 128
-                local = head_ids[q] - start
-                missing = jnp.logical_or(local < 0, local >= ents)
-                rows.append(tab[pl.ds(jnp.where(missing, ents, local), 1), :])
-            out[k, pl.ds(pl.multiple_of(i * 8, 8), 8), :] = jnp.concatenate(rows, axis=0)
+        for part in range(2):
+            base = k * 512 + part * 256 + half * 128
+
+            @pl.loop(0, 16)
+            def _(i):
+                rows = []
+                for j in range(8):
+                    local = (head_ids[base + i * 8 + j] - start).astype(jnp.uint32)
+                    row = jnp.minimum(local, jnp.uint32(ents)).astype(jnp.int32)
+                    rows.append(tab[pl.ds(row, 1), :])
+                span = pl.ds(pl.multiple_of(part * 128 + i * 8, 8), 8)
+                out[k, span, :] = jnp.concatenate(rows, axis=0)
 
     order = [(x + 2) % 4, (x + 1) % 4, (x + 3) % 4, x]
     copies, x_copies = [], {}
@@ -130,11 +139,12 @@
         span = pl.ds(pl.multiple_of(i * 256, 256), 256)
         ent[span, :] = tab[span, :].astype(jnp.bfloat16)
 
+    for copy in small[1:]:
+        copy.wait()
     found = jnp.zeros(level.shape, F32)
     for k in range(thresholds.shape[0]):
         found = jnp.where(thr_idx[...] == k, thresholds[k], found)
     level[...] = found
-    load_rel.wait()
     first_q = r * 128 + d * 16
     for i in range(16):
         rel_rows[pl.ds(i, 1), :] = rel[pl.ds(rel_ids[first_q + i], 1), :]
@@ -171,9 +181,15 @@
         gath_copies[i].wait_recv()
 
     xg_copies = {}
-    for k in (1, 3, 2):
-        xg_copies[k] = send(queries.at[own_group], queries.at[own_group], xg_send.at[k - 1], xg_recv.at[k - 1], at_x(k))
-
+
+    def gather_x(k):
+        xg_copies[k] = send(
+            queries.at[own_group], queries.at[own_group], xg_send.at[k - 1], xg_recv.at[k - 1], at_x(k)
+        )
+
+    gather_x(1)
+    gather_x(3)
+    start_wave(3)
     tile = 512
 
     def count(half, k):
@@ -192,15 +208,31 @@
         totals[g] = lax.fori_loop(0, ents // tile, step, jnp.zeros((8, group), F32))
 
     pg_copies = []
-    for n, k in enumerate((0, 1, 3, 2)):
+
+    def pass_on(n, k):
+        g = core * 4 + (x + 4 - k) % 4
+        pg_copies.append(send(queries.at[g], queries.at[g], pg_send.at[n], pg_recv.at[n], partner))
+
+    def both(n, k):
         from_x = (x + 4 - k) % 4
-        if k:
-            xg_copies[k].wait_recv()
-        g = core * 4 + from_x
-        pg_copies.append(send(queries.at[g], queries.at[g], pg_send.at[n], pg_recv.at[n], partner))
         count(core, from_x)
+        start_wave(4 + 2 * n)
         pg_copies[n].wait_recv()
         count(1 - core, from_x)
+        start_wave(5 + 2 * n)
+
+    pass_on(0, 0)
+    both(0, 0)
+    xg_copies[1].wait_recv()
+    xg_copies[3].wait_recv()
+    gather_x(2)
+    pass_on(1, 1)
+    pass_on(2, 3)
+    both(1, 1)
+    both(2, 3)
+    xg_copies[2].wait_recv()
+    pass_on(3, 2)
+    both(3, 2)
 
     other = pl.ds((1 - core) * 4, 4)
     half = send(totals.at[other], pair_tot, tot_send.at[0], tot_recv.at[0], partner)
@@ -223,7 +255,7 @@
         plane_tots.append(
             send(plane_tot.at[(row // 2) % 2], plane_tot.at[2 + i], tot_send.at[4 + i], tot_recv.at[4 + i], (row, col))
         )
-    start_wave(3)
+    start_wave(12)
     whole = plane_tot[y_lo]
     for i in range(15):
         plane_tots[i].wait_recv()
@@ -256,7 +288,6 @@
     slab = width // n_dim
     group = 256
     hbm = pl.BlockSpec(memory_space=pl.ANY)
-    smem = pl.BlockSpec(memory_space=pltpu.SMEM)
     vmem = pl.BlockSpec(memory_space=pltpu.VMEM)
     dma = pltpu.SemaphoreType.DMA
     waves = len(WAVES)
@@ -266,9 +297,13 @@
             pltpu.VMEM((slab, ents * n_dim), F32),
             pltpu.VMEM((8, 128), F32),
         ),
-        in_specs=[smem, smem, smem, hbm, hbm, vmem],
+        in_specs=[hbm] * 6,
         out_specs=(vmem, vmem),
         scratch_shapes=[
+            pltpu.SMEM(head_ids.shape, jnp.int32),
+            pltpu.SMEM(rel_ids.shape, jnp.int32),
+            pltpu.SMEM(thresholds.shape, F32),
+            pltpu.VMEM((16, 128), jnp.int32),
             pltpu.VMEM((ents + 8, width), F32),
             pltpu.VMEM((width, ents), F32),
             pltpu.VMEM((ents, width), jnp.bfloat16),
@@ -286,7 +321,7 @@
             pltpu.VMEM((4, 8, group), F32),
             pltpu.VMEM((7, 8, group), F32),
             pltpu.VMEM((17, 8, 128), F32),
-            dma((5,)),
+            dma((9,)),
             dma((waves, 7)), dma((waves, 7)),
             dma((4,)), dma((4,)),
             dma((3,)), dma((3,)),

time: 136 us -> 124 us (0.912); the launches traced: 133 us -> 123 us
  Pallas kernels: 132 us -> 122 us
    pallas_call x1, Pallas kernels: 128 us -> 119 us  [shards(): pl.pallas_call(functools.partial(kernel, total_ents), out_shape=(pltpu.VM...]
where the time goes in v3:
time: 124 us; the launch traced here: 123 us
  Pallas kernels  122 us (98%)
    pallas_call x1, Pallas kernels, shards(): pl.pallas_call(functools.partial(kernel, total_ents), out_shape=(pltpu.VM...  119 us
    pallas_call x1, Pallas kernels, shards(): pl.pallas_call(write_out, out_shape=(jax.ShapeDtypeStruct((slab, ents * n...  3.88 us

profile of v3, /device:TPU:1, one launch (start us, length us, event | category | flops | bytes accessed | tf_op | source)
XLA Modules:
  0.0 123.1 jit_solution(1758351621730873104)
XLA Ops:
  0.6 118.6 %serve_and_count.1 = (f32[64,32768]{1,0:T(8,128)S(1)}, f32[8,128]{1,0:T(8,128)S(1)}) custom-call(s32[2048]{0:T(1024)} %head_ids_in.1, s32[2048]{0:T(1024)} %rel_ids_in.1, f32[64]{0:T(128)} %thresholds_in.1, f32[4096,512]{1,0:T(8,128)} %table.1, f32[822,512]{1,0:T(8,128)} %relations.1, s32[16,128]{1,0:T(8,128)} %bitcast.2), custom_call_target="tpu_custom_call" | custom-call | tf_op jit(solution)/shard_map/serve_and_count/pallas_call | solution.py:294
  119.2 3.9 %write_out.1 = (f32[64,32768]{1,0:T(8,128)}, f32[16]{0:T(128)}) custom-call(f32[64,32768]{1,0:T(8,128)S(1)} %get-tuple-element.6.landed, f32[8,128]{1,0:T(8,128)S(1)} %get-tuple-element.7.share), custom_call_target="tpu_custom_call" | custom-call | tf_op jit(solution)/shard_map/write_out/pallas_call | solution.py:339

commit v4 on v3

--- a/solution.py
+++ b/solution.py
@@ -25,7 +25,7 @@
     level, totals, pair_tot, x_tot, plane_tot,
     load_sem, slab_send, slab_recv, pair_send, pair_recv, x_send, x_recv,
     plane_send, plane_recv, gath_send, gath_recv, xg_send, xg_recv, pg_send, pg_recv,
-    tot_send, tot_recv,
+    tot_send, tot_recv, last_send, last_recv,
 ):
     r, d = lax.axis_index("rows"), lax.axis_index("dim")
     x, y_lo, core = r // 4, (r // 2) % 2, r % 2
@@ -51,6 +51,11 @@
         )
         copy.start()
         return copy
+
+    def all_of(src, dst, s, t):
+        return pltpu.make_async_remote_copy(
+            src_ref=src, dst_ref=dst, send_sem=s, recv_sem=t, device_id=partner, device_id_type=MESH
+        )
 
     cuts = [0, COUNTS[0], 2048, 3072, ents]
     loads = []
@@ -75,18 +80,14 @@
             span = pl.ds(pl.multiple_of(first + i * 128, 128), 128)
             tab_t[:, span] = tab[span, :].T
 
-    slab_copies = []
-
     def start_wave(w):
         first, count = WAVES[w]
         span = pl.ds(first, count)
         here = pl.ds(pl.multiple_of(d * ents + first, 128), count)
-        for i, off in enumerate(SLABS):
+        for off in SLABS:
             row, col = at_plane(off)
             rows = pl.ds(pl.multiple_of(col * slab, 8), slab)
-            slab_copies.append(
-                send(tab_t.at[rows, span], serving.at[:, here], slab_send.at[w, i], slab_recv.at[w, i], (row, col))
-            )
+            send(tab_t.at[rows, span], serving.at[:, here], slab_send, slab_recv, (row, col))
         rows = pl.ds(pl.multiple_of(d * slab, 8), slab)
         serving[:, here] = tab_t[rows, span]
 
@@ -156,29 +157,23 @@
     def rows_of(row, col):
         return pl.ds(pl.multiple_of(((row // 2) % 2) * 128 + col * 16, 16), 16)
 
-    plane_copies = []
     for i, off in enumerate(PLANE):
         peer = at_plane(off)
-        plane_copies.append(
-            send(mine.at[x, rows_of(*peer)], plane_in.at[i], plane_send.at[i], plane_recv.at[i], peer)
-        )
+        send(mine.at[x, rows_of(*peer)], plane_in.at[i], plane_send, plane_recv, peer)
     start_wave(1)
     head = mine[x, rows_of(r, d)]
+    all_of(mine.at[x, pl.ds(0, 240)], plane_in, plane_send, plane_recv).wait_recv()
     for i in range(15):
-        plane_copies[i].wait_recv()
         head += plane_in[i]
 
     query_rows[...] = (head * rel_rows[...]).astype(jnp.bfloat16).astype(F32)
     own_group = core * 4 + x
-    gath_copies = []
-    for i, off in enumerate(PLANE):
-        gath_copies.append(
-            send(query_rows, queries.at[own_group, rows_of(r, d)], gath_send.at[i], gath_recv.at[i], at_plane(off))
-        )
+    for off in PLANE:
+        send(query_rows, queries.at[own_group, rows_of(r, d)], gath_send, gath_recv, at_plane(off))
     start_wave(2)
     queries[own_group, rows_of(r, d)] = query_rows[...]
-    for i in range(15):
-        gath_copies[i].wait_recv()
+    gathered = all_of(mine.at[x, pl.ds(0, 240)], queries.at[own_group, pl.ds(0, 240)], gath_send, gath_recv)
+    gathered.wait_recv()
 
     xg_copies = {}
 
@@ -233,6 +228,11 @@
     xg_copies[2].wait_recv()
     pass_on(3, 2)
     both(3, 2)
+
+    for copy in copies + list(x_copies.values()) + list(xg_copies.values()) + pg_copies:
+        copy.wait_send()
+    all_of(mine.at[x, pl.ds(0, 240)], plane_in, plane_send, plane_recv).wait_send()
+    gathered.wait_send()
 
     other = pl.ds((1 - core) * 4, 4)
     half = send(totals.at[other], pair_tot, tot_send.at[0], tot_recv.at[0], partner)
@@ -249,25 +249,25 @@
         sums += x_tot[3 + k]
     plane_tot[0] = sums[:, :128]
     plane_tot[1] = sums[:, 128:]
-    plane_tots = []
     for i, off in enumerate(PLANE):
         row, col = at_plane(off)
-        plane_tots.append(
-            send(plane_tot.at[(row // 2) % 2], plane_tot.at[2 + i], tot_send.at[4 + i], tot_recv.at[4 + i], (row, col))
-        )
+        send(plane_tot.at[(row // 2) % 2], plane_tot.at[2 + i], last_send, last_recv, (row, col))
     start_wave(12)
     whole = plane_tot[y_lo]
+    last = all_of(plane_tot.at[pl.ds(0, 15)], plane_tot.at[pl.ds(2, 15)], last_send, last_recv)
+    last.wait_recv()
+    half.wait_send()
+    for k in (1, 2, 3):
+        x_tots[k].wait_send()
     for i in range(15):
-        plane_tots[i].wait_recv()
         whole += plane_tot[2 + i]
     whole = jnp.sum(whole, axis=0, keepdims=True) * (1.0 / total_ents)
     share[...] = pltpu.roll(jnp.broadcast_to(whole, (8, 128)), (128 - d * 16) % 128, 1)
 
-    for copy in slab_copies:
-        copy.wait_recv()
-    sent = copies + list(x_copies.values()) + plane_copies + gath_copies + list(xg_copies.values())
-    for copy in sent + pg_copies + [half] + list(x_tots.values()) + plane_tots + slab_copies:
-        copy.wait_send()
+    slabs = all_of(tab_t.at[pl.ds(0, 7 * slab)], serving.at[:, pl.ds(0, 7 * ents)], slab_send, slab_recv)
+    slabs.wait_recv()
+    slabs.wait_send()
+    last.wait_send()
 
 
 def write_out(landed, share, serving, fraction, sems):
@@ -290,7 +290,6 @@
     hbm = pl.BlockSpec(memory_space=pl.ANY)
     vmem = pl.BlockSpec(memory_space=pltpu.VMEM)
     dma = pltpu.SemaphoreType.DMA
-    waves = len(WAVES)
     landed, share = pl.pallas_call(
         functools.partial(kernel, total_ents),
         out_shape=(
@@ -322,14 +321,15 @@
             pltpu.VMEM((7, 8, group), F32),
             pltpu.VMEM((17, 8, 128), F32),
             dma((9,)),
-            dma((waves, 7)), dma((waves, 7)),
+            dma, dma,
             dma((4,)), dma((4,)),
             dma((3,)), dma((3,)),
-            dma((15,)), dma((15,)),
-            dma((15,)), dma((15,)),
+            dma, dma,
+            dma, dma,
             dma((3,)), dma((3,)),
             dma((4,)), dma((4,)),
-            dma((19,)), dma((19,)),
+            dma((4,)), dma((4,)),
+            dma, dma,
         ],
         compiler_params=pltpu.CompilerParams(
             collective_id=0, has_side_effects=True, vmem_limit_bytes=48 * 1024 * 1024

time: 124 us -> 121 us (0.976)
  Pallas kernels: 122 us -> 120 us
    pallas_call x1, Pallas kernels: 119 us -> 116 us  [shards(): pl.pallas_call(functools.partial(kernel, total_ents), out_shape=(pltpu.VM...]
where the time goes in v4:
time: 121 us; the launch traced here: 120 us
  Pallas kernels  120 us (99%)
    pallas_call x1, Pallas kernels, shards(): pl.pallas_call(functools.partial(kernel, total_ents), out_shape=(pltpu.VM...  116 us
    pallas_call x1, Pallas kernels, shards(): pl.pallas_call(write_out, out_shape=(jax.ShapeDtypeStruct((slab, ents * n...  3.88 us

profile of v4, /device:TPU:1, one launch (start us, length us, event | category | flops | bytes accessed | tf_op | source)
XLA Modules:
  0.0 120.5 jit_solution(6912913316218643667)
XLA Ops:
  0.6 115.9 %serve_and_count.1 = (f32[64,32768]{1,0:T(8,128)S(1)}, f32[8,128]{1,0:T(8,128)S(1)}) custom-call(s32[2048]{0:T(1024)} %head_ids_in.1, s32[2048]{0:T(1024)} %rel_ids_in.1, f32[64]{0:T(128)} %thresholds_in.1, f32[4096,512]{1,0:T(8,128)} %table.1, f32[822,512]{1,0:T(8,128)} %relations.1, s32[16,128]{1,0:T(8,128)} %bitcast.2), custom_call_target="tpu_custom_call" | custom-call | tf_op jit(solution)/shard_map/serve_and_count/pallas_call | solution.py:293
  116.6 3.9 %write_out.1 = (f32[64,32768]{1,0:T(8,128)}, f32[16]{0:T(128)}) custom-call(f32[64,32768]{1,0:T(8,128)S(1)} %get-tuple-element.6.landed, f32[8,128]{1,0:T(8,128)S(1)} %get-tuple-element.7.share), custom_call_target="tpu_custom_call" | custom-call | tf_op jit(solution)/shard_map/write_out/pallas_call | solution.py:339

commit v5 on v4

--- a/solution.py
+++ b/solution.py
@@ -13,7 +13,7 @@
 
 PLANE = [(a, b, z) for a in range(2) for b in range(2) for z in range(4)][1:]
 SLABS = [(0, 1, 2), (0, 0, 2), (0, 1, 1), (0, 1, 3), (0, 1, 0), (0, 0, 1), (0, 0, 3)]
-COUNTS = [1152, 256, 256, 768, 128, 256, 128, 128, 256, 128, 128, 256, 256]
+COUNTS = [1152, 256, 256, 896, 128, 128, 256, 128, 128, 256, 128, 128, 256]
 WAVES = [(sum(COUNTS[:k]), COUNTS[k]) for k in range(len(COUNTS))]
 
 

time: 121 us -> 120 us (level)
  no operation moved by 1% of the time
where the time goes in v5:
time: 120 us
  Pallas kernels  119 us (99%)
    pallas_call x1, Pallas kernels, shards(): pl.pallas_call(functools.partial(kernel, total_ents), out_shape=(pltpu.VM...  115 us
    pallas_call x1, Pallas kernels, shards(): pl.pallas_call(write_out, out_shape=(jax.ShapeDtypeStruct((slab, ents * n...  3.88 us

profile of v5, /device:TPU:1, one launch (start us, length us, event | category | flops | bytes accessed | tf_op | source)
XLA Modules:
  0.0 120.0 jit_solution(11744559913034063293)
XLA Ops:
  0.6 115.5 %serve_and_count.1 = (f32[64,32768]{1,0:T(8,128)S(1)}, f32[8,128]{1,0:T(8,128)S(1)}) custom-call(s32[2048]{0:T(1024)} %head_ids_in.1, s32[2048]{0:T(1024)} %rel_ids_in.1, f32[64]{0:T(128)} %thresholds_in.1, f32[4096,512]{1,0:T(8,128)} %table.1, f32[822,512]{1,0:T(8,128)} %relations.1, s32[16,128]{1,0:T(8,128)} %bitcast.2), custom_call_target="tpu_custom_call" | custom-call | tf_op jit(solution)/shard_map/serve_and_count/pallas_call | solution.py:293
  116.1 3.9 %write_out.1 = (f32[64,32768]{1,0:T(8,128)}, f32[16]{0:T(128)}) custom-call(f32[64,32768]{1,0:T(8,128)S(1)} %get-tuple-element.6.landed, f32[8,128]{1,0:T(8,128)S(1)} %get-tuple-element.7.share), custom_call_target="tpu_custom_call" | custom-call | tf_op jit(solution)/shard_map/write_out/pallas_call | solution.py:339

commit v6 on v5

--- a/solution.py
+++ b/solution.py
@@ -57,7 +57,7 @@
             src_ref=src, dst_ref=dst, send_sem=s, recv_sem=t, device_id=partner, device_id_type=MESH
         )
 
-    cuts = [0, COUNTS[0], 2048, 3072, ents]
+    cuts = [0, 512, COUNTS[0], 2560, ents]
     loads = []
     for k in range(4):
         span = pl.ds(cuts[k], cuts[k + 1] - cuts[k])
@@ -92,10 +92,12 @@
         serving[:, here] = tab_t[rows, span]
 
     loads[0].wait()
-    transpose_rows(*WAVES[0])
+    transpose_rows(0, cuts[1])
+    loads[1].wait()
+    transpose_rows(cuts[1], cuts[2] - cuts[1])
     pl.semaphore_wait(barrier, len(peers))
     start_wave(0)
-    for k in range(1, 4):
+    for k in range(2, 4):
         loads[k].wait()
     small[0].wait()
 

time: 120 us -> 120 us (level)
  no operation moved by 1% of the time
where the time goes in v6:
time: 120 us
  Pallas kernels  119 us (99%)
    pallas_call x1, Pallas kernels, shards(): pl.pallas_call(functools.partial(kernel, total_ents), out_shape=(pltpu.VM...  115 us
    pallas_call x1, Pallas kernels, shards(): pl.pallas_call(write_out, out_shape=(jax.ShapeDtypeStruct((slab, ents * n...  3.88 us

profile of v6, /device:TPU:1, one launch (start us, length us, event | category | flops | bytes accessed | tf_op | source)
XLA Modules:
  0.0 120.0 jit_solution(8717550765116701893)
XLA Ops:
  0.6 115.5 %serve_and_count.1 = (f32[64,32768]{1,0:T(8,128)S(1)}, f32[8,128]{1,0:T(8,128)S(1)}) custom-call(s32[2048]{0:T(1024)} %head_ids_in.1, s32[2048]{0:T(1024)} %rel_ids_in.1, f32[64]{0:T(128)} %thresholds_in.1, f32[4096,512]{1,0:T(8,128)} %table.1, f32[822,512]{1,0:T(8,128)} %relations.1, s32[16,128]{1,0:T(8,128)} %bitcast.2), custom_call_target="tpu_custom_call" | custom-call | tf_op jit(solution)/shard_map/serve_and_count/pallas_call | solution.py:295
  116.1 3.9 %write_out.1 = (f32[64,32768]{1,0:T(8,128)}, f32[16]{0:T(128)}) custom-call(f32[64,32768]{1,0:T(8,128)S(1)} %get-tuple-element.6.landed, f32[8,128]{1,0:T(8,128)S(1)} %get-tuple-element.7.share), custom_call_target="tpu_custom_call" | custom-call | tf_op jit(solution)/shard_map/write_out/pallas_call | solution.py:341
